TPU v7x, 32 devices: a whole 2x2x4 slice. The times are simulated.
32 devices in a mesh: dp: 4 (over x, core), tensor: 8 (over z, y).
Axes of the slice: x: 2, y: 2, z: 4, core: 2. Of those that a mesh axis runs over, the one named last changes fastest.
Arguments:
- activations: bfloat16 [2048, 28672], P('dp', 'tensor'), parts along dimension 0, may hold values from -6 to 6
- down_weight: bfloat16 [28672, 6144], P('tensor'), may hold values from -0.046875 to 0.046875
Outputs:
- projected: bfloat16 [2048, 6144], P(('dp', 'tensor')), parts along dimension 0
There are 4 independent parts, one for each index of `dp`. A program takes and returns all parts, laid end to end along the dimension named above; an argument that names none is the same for every part. Nothing has to cross between parts.
All inputs are finite; a program needn't handle non-finite values.
Results may differ from a plain program's by a relative error of at most 0.015.
Values may be sent and summed in bfloat16 or wider, within the bound.
A program may use at most 128 MiB of HBM per device.

v0:
```python
import math

import jax
import jax.numpy as jnp
import numpy as np
from jax import lax
from jax.sharding import PartitionSpec as P


def paley_matrix():
    modulus = 13
    residues = set((value * value % modulus for value in range(1, modulus)))
    jacobsthal = np.array(
        [
            [
                (
                    0.0
                    if row_at == col_at
                    else 1.0 if (col_at - row_at) % modulus in residues else -1.0
                )
                for col_at in range(modulus)
            ]
            for row_at in range(modulus)
        ]
    )
    confer = np.zeros((14, 14))
    confer[0, 1:] = 1.0
    confer[1:, 0] = 1.0
    confer[1:, 1:] = jacobsthal
    return np.kron(confer, np.array([[1.0, 1.0], [1.0, -1.0]])) + np.kron(
        np.eye(14), np.array([[1.0, -1.0], [-1.0, -1.0]])
    )


def sylvester(order):
    matrix = np.ones((1, 1))
    while matrix.shape[0] < order:
        matrix = np.kron(matrix, np.array([[1.0, 1.0], [1.0, -1.0]]))
    return matrix


def quantize(rotated, largest):
    token_scale = jnp.maximum(largest, 1.0)
    levels = 7.0 * rotated / token_scale
    snapped = levels - jnp.sin(2.0 * math.pi * levels) / (2.0 * math.pi)
    return (snapped * token_scale / 7.0).astype(jnp.bfloat16)


def shards(activations, down_weight):
    count_rows, shard_width = activations.shape
    groups = lax.axis_size("tensor")
    local_order = shard_width // 28
    rotation = jnp.asarray(np.kron(sylvester(local_order), paley_matrix()), jnp.bfloat16)
    mixed_rows = jnp.dot(activations, rotation, preferred_element_type=jnp.float32)
    normal_scale = 1.0 / math.sqrt(shard_width * groups)
    cross_table = jnp.asarray(sylvester(groups), jnp.float32)
    blocks = mixed_rows.reshape(groups, count_rows // groups, shard_width)
    rotated = (
        jnp.einsum(
            "ea,etf->atf",
            cross_table,
            lax.all_to_all(blocks, "tensor", split_axis=0, concat_axis=0, tiled=True),
            precision=lax.Precision.HIGHEST,
        )
        * normal_scale
    )
    largest = jnp.max(jnp.abs(rotated), axis=(0, 2), keepdims=True)
    returned = lax.all_to_all(
        quantize(rotated, largest), "tensor", split_axis=0, concat_axis=0, tiled=True
    )
    dequant = returned.reshape(count_rows, shard_width)
    return lax.psum_scatter(
        jnp.dot(dequant, down_weight, preferred_element_type=jnp.float32).astype(jnp.bfloat16),
        "tensor",
        scatter_dimension=0,
        tiled=True,
    )


def solution(mesh):
    placed = (P("dp", "tensor"), P("tensor", None))
    return jax.shard_map(
        shards, mesh=mesh, in_specs=placed, out_specs=P(("dp", "tensor"), None), check_vma=False
    )
```

profile of v0, /device:TPU:0, one launch (start us, length us, event | category | flops | bytes accessed | tf_op | source)
XLA Modules:
  0.0 473.5 jit_solution(2288884644030211940)
XLA Ops:
  6.5 0.0 reduce-scatter.2.cloned.1.call-start
  6.5 19.4 %fusion.7 = f32[3584,512]{0,1:T(8,128)S(1)} fusion(bf16[512,3584]{1,0:T(8,128)(2,1)} %param.4, bf16[3584,3584]{1,0:T(8,128)(2,1)} %constant.19.clone), kind=kOutput, calls=%fused_computation.12 | convolution fusion | flops 13153337344 | bytes 36700160 | tf_op jit(solution)/shard_map/dot_general | solution.py:54
  25.9 0.0 copy-start
  26.0 167.7 %all_to_all.10 = f32[8,64,3584]{2,1,0:T(8,128)S(1)} all-to-all(f32[8,64,3584]{2,1,0:T(8,128)S(1)} %bitcast.25), channel_id=1, replica_groups=mesh['dp'=4,'tensor'=8] {'tensor'}, dimensions={0} | all-to-all | bytes 14680064 | tf_op jit(solution)/shard_map/all_to_all | solution.py:62
  193.7 0.0 copy-done
  193.7 12.8 %abs_reduce_fusion = (f32[64]{0:T(128)S(1)}, f32[64,3584,8]{1,2,0:T(8,128)S(1)}) fusion(f32[8,8,1]{0,1,2:T(8,128)S(1)} %copy-done, f32[8,64,3584]{2,1,0:T(8,128)S(1)} %all_to_all.10), kind=kOutput, calls=%fused_computation.10 | convolution fusion | flops 181665728 | bytes 14680576 | tf_op jit(solution)/shard_map/ea,etf->atf/dot_general | solution.py:59
  206.5 26.5 %fusion.4 = bf16[8,64,3584]{2,0,1:T(8,128)(2,1)S(1)} fusion(f32[64,3584,8]{1,2,0:T(8,128)S(1)} %get-tuple-element.6, f32[64]{0:T(128)S(1)} %broadcast_maximum_fusion), kind=kLoop, calls=%fused_computation.7 | loop fusion | flops 14680064 | bytes 11010304 | tf_op jit(solution)/shard_map/convert_element_type | solution.py:46
  233.0 1.1 copy.9
  234.1 85.2 %all_to_all.11 = bf16[8,64,3584]{2,1,0:T(8,128)(2,1)S(1)} all-to-all(bf16[8,64,3584]{2,1,0:T(8,128)(2,1)S(1)} %copy.9), channel_id=1, replica_groups=mesh['dp'=4,'tensor'=8] {'tensor'}, dimensions={0} | all-to-all | bytes 7340032 | tf_op jit(solution)/shard_map/all_to_all | solution.py:68
  319.3 30.4 %convolution_convert_fusion = bf16[512,6144]{1,0:T(8,128)(2,1)} fusion(bf16[512,3584]{1,0:T(8,128)(2,1)S(1)} %bitcast.26, bf16[3584,6144]{1,0:T(8,128)(2,1)} %param.5), kind=kOutput, calls=%fused_computation | convolution fusion | flops 22551724032 | bytes 54001664 | tf_op jit(solution)/shard_map/dot_general | solution.py:73
  349.7 0.0 reduce-scatter.2.cloned.1.call-update
  349.7 117.0 %reduce-scatter.2.cloned.1.call-done = bf16[64,6144]{1,0:T(8,128)(2,1)} async-done(((bf16[512,6144]{1,0:T(8,128)(2,1)}), bf16[64,6144]{1,0:T(8,128)(2,1)}) %reduce-scatter.2.cloned.1.call-update) | async-done | bytes 786448 | tf_op jit(solution)/shard_map/reduce_scatter | solution.py:72
  (1 shorter events, 0.0 us)
Async XLA Ops:
  6.5 460.2 %reduce-scatter.2.cloned.1.call-start = ((), (), s32[]{:S(2)}) async-start(), calls=%async_computation.3 | async-start | bytes 7077888 | tf_op jit(solution)/shard_map/reduce_scatter | solution.py:72
  25.9 167.7 %copy-start = (f32[8,8,1]{0,1,2:T(8,128)S(1)}, f32[8,8,1]{0,1,2:T(8,128)}, u32[]{:S(2)}) copy-start(f32[8,8,1]{0,1,2:T(8,128)} %constant.21) | copy-start | bytes 772
Sparse Core Ops, SparseCore 0:
  349.8 116.8 reduce-scatter.1
where the time goes:
time: 474 us
  blocking collectives  253 us (53%)
  waiting for transfers between devices  117 us (25%)
  matrix products  62.6 us (13%)
  other arithmetic  26.5 us (6%)
  between operations  13.4 us (3%)
    all_to_all x1, blocking collectives, shards(): lax.all_to_all(blocks, 'tensor', split_axis=0, concat_axis=0, tiled=True)  168 us
    reduce_scatter x1, waiting for transfers between devices, shards(): lax.psum_scatter(jnp.dot(dequant, down_weight, preferred_element_type=jnp...  117 us
    all_to_all x1, blocking collectives, shards(): lax.all_to_all(quantize(rotated, largest), 'tensor', split_axis=0, concat...  85.2 us
    dot_general x1, matrix products, shards(): jnp.dot(dequant, down_weight, preferred_element_type=jnp.float32)  30.4 us
    convert_element_type x1, other arithmetic, quantize(): return (snapped * token_scale / 7.0).astype(jnp.bfloat16)  26.5 us
    dot_general x1, matrix products, shards(): jnp.dot(activations, rotation, preferred_element_type=jnp.float32)  19.4 us
    dot_general x1, matrix products, shards(): jnp.einsum('ea,etf->atf', cross_table, lax.all_to_all(blocks, 'tensor', s...  12.8 us
  transfers between devices with their start and end apart: 1, of which 1 were waited for; matrix products, arithmetic and copies ran while one was open for 0% of the time, Pallas kernels for 0%

commit v1 on v0

v1 whole, which is shorter than its diff:
```python
import functools
import math

import jax
import jax.numpy as jnp
import numpy as np
from jax import lax
from jax.experimental import pallas as pl
from jax.experimental.pallas import tpu as pltpu
from jax.sharding import PartitionSpec as P

INNER = 32
WEIGHT_SLOTS = 3


def paley_matrix():
    modulus = 13
    residues = set((value * value % modulus for value in range(1, modulus)))
    jacobsthal = np.array(
        [
            [
                (
                    0.0
                    if row_at == col_at
                    else 1.0 if (col_at - row_at) % modulus in residues else -1.0
                )
                for col_at in range(modulus)
            ]
            for row_at in range(modulus)
        ]
    )
    confer = np.zeros((14, 14))
    confer[0, 1:] = 1.0
    confer[1:, 0] = 1.0
    confer[1:, 1:] = jacobsthal
    return np.kron(confer, np.array([[1.0, 1.0], [1.0, -1.0]])) + np.kron(
        np.eye(14), np.array([[1.0, -1.0], [-1.0, -1.0]])
    )


def sylvester(order):
    matrix = np.ones((1, 1))
    while matrix.shape[0] < order:
        matrix = np.kron(matrix, np.array([[1.0, 1.0], [1.0, -1.0]]))
    return matrix


def sine_terms():
    series = np.polynomial.chebyshev.Chebyshev.interpolate(
        lambda square: np.sinc(2.0 * np.sqrt(np.maximum(square, 0.0))), 8, domain=[0.0, 0.25]
    )
    power = series.convert(kind=np.polynomial.Polynomial, domain=[-1, 1], window=[-1, 1])
    return [float(value) for value in power.coef]


def butterfly(values):
    step = 1
    while step < len(values):
        result = list(values)
        for at in range(len(values)):
            if not at & step:
                result[at] = values[at] + values[at + step]
                result[at + step] = values[at] - values[at + step]
        values, step = result, step * 2
    return values


def flipped(position, mask):
    result, bit = position, 1
    while bit <= mask:
        if mask & bit:
            result = result + (1 - 2 * ((position // bit) % 2)) * bit
        bit *= 2
    return result


def mirrored(position, groups):
    result, bit = 0, 1
    while bit < groups:
        result = result + ((position // bit) % 2) * (groups // 2 // bit)
        bit *= 2
    return result


def kernel(
    groups, chunks, tile, normal_scale, terms,
    act_ref, weight_ref, table_ref, out_ref,
    x_buf, rot, q_buf, d_buf, part, w_buf, *rest,
):
    stages = groups.bit_length() - 1
    recv_bufs = rest[:stages]
    (x_send, x_recv, own_sem, q_send, q_recv, r_send, r_recv, w_sem) = rest[stages:]
    me = lax.axis_index("tensor")
    rows = x_buf.shape[2]
    width = x_buf.shape[3]
    inner = table_ref.shape[0]
    subs = width // inner
    tiles = weight_ref.shape[1] // tile
    place = mirrored(me, groups)
    peers = [(mask, flipped(me, mask)) for mask in range(groups - 1, 0, -1)]

    def weight_copy(step):
        column = pl.multiple_of((step % tiles) * tile, 128)
        slot = step % WEIGHT_SLOTS
        return pltpu.make_async_copy(
            weight_ref.at[:, pl.ds(column, tile)], w_buf.at[slot], w_sem.at[slot]
        )

    def own_rows(chunk):
        first = pl.multiple_of(me * (chunks * rows) + chunk * rows, rows)
        return pltpu.make_async_copy(
            act_ref.at[pl.ds(first, rows), :], x_buf.at[chunk, me], own_sem.at[chunk]
        )

    def x_copy(chunk, mask, peer):
        first = pl.multiple_of(peer * (chunks * rows) + chunk * rows, rows)
        return pltpu.make_async_remote_copy(
            src_ref=act_ref.at[pl.ds(first, rows), :],
            dst_ref=x_buf.at[chunk, me],
            send_sem=x_send.at[chunk, mask],
            recv_sem=x_recv.at[chunk, mask],
            device_id={"tensor": peer},
            device_id_type=pl.DeviceIdType.MESH,
        )

    def q_copy(chunk, mask, peer):
        return pltpu.make_async_remote_copy(
            src_ref=q_buf.at[chunk, peer],
            dst_ref=d_buf.at[chunk, place],
            send_sem=q_send.at[chunk, mask],
            recv_sem=q_recv.at[chunk, mask],
            device_id={"tensor": peer},
            device_id_type=pl.DeviceIdType.MESH,
        )

    def half_at(stage):
        start, span, kept = 0, groups, 0
        for at in range(stage + 1):
            span //= 2
            start = kept
            bit = (me // (1 << at)) % 2
            kept = start + bit * span
            sent = start + (1 - bit) * span
        return kept, sent, span

    def r_copy(chunk, stage):
        kept, sent, span = half_at(stage)
        return pltpu.make_async_remote_copy(
            src_ref=part.at[chunk, pl.ds(sent, span)],
            dst_ref=recv_bufs[stage].at[chunk],
            send_sem=r_send.at[chunk, stage],
            recv_sem=r_recv.at[chunk, stage],
            device_id={"tensor": flipped(me, 1 << stage)},
            device_id_type=pl.DeviceIdType.MESH,
        )

    barrier = pltpu.get_barrier_semaphore()
    for mask, peer in peers:
        pl.semaphore_signal(
            barrier, inc=1, device_id={"tensor": peer}, device_id_type=pl.DeviceIdType.MESH
        )
    pl.semaphore_wait(barrier, groups - 1)

    for chunk in range(chunks):
        for mask, peer in peers:
            x_copy(chunk, mask, peer).start()
        own_rows(chunk).start()
    for step in range(WEIGHT_SLOTS):
        weight_copy(step).start()

    @pl.loop(0, chunks)
    def _(chunk):
        own_rows(chunk).wait()
        for mask, peer in peers:
            x_copy(chunk, mask, peer).wait_recv()
        for sub in range(subs):
            block = x_buf[chunk, :, :, sub * inner:(sub + 1) * inner]
            rot[sub] = jnp.dot(
                block.reshape(groups * rows, inner), table_ref[...],
                preferred_element_type=jnp.float32,
            ).reshape(groups, rows, inner)

        def mix(at, tops):
            column = pl.ds(pl.multiple_of(at * 128, 128), 128)
            result = []
            for index in range(rows // 8):
                line = pl.ds(index * 8, 8)
                values = butterfly(
                    [rot[sub, group, line, column] for group in range(groups) for sub in range(subs)]
                )
                top = tops[index]
                for block_at, value in enumerate(values):
                    rot[block_at % subs, block_at // subs, line, column] = value
                    top = jnp.maximum(top, jnp.abs(value))
                result.append(top)
            return tuple(result)

        tops = lax.fori_loop(
            0, inner // 128, mix,
            tuple(jnp.zeros((8, 128), jnp.float32) for _ in range(rows // 8)),
        )
        largest = jnp.concatenate([jnp.max(top, axis=1, keepdims=True) for top in tops], axis=0)
        token_scale = jnp.maximum(largest * normal_scale, 1.0)
        into = 7.0 * normal_scale / token_scale
        back = token_scale / 7.0

        @pl.loop(0, groups)
        def _(group):
            for sub in range(subs):
                levels = rot[sub, group] * into
                offset = levels - jnp.floor(levels + 0.5)
                square = offset * offset
                series = jnp.full_like(square, terms[-1])
                for term in terms[-2::-1]:
                    series = series * square + term
                q_buf[chunk, group, :, sub * inner:(sub + 1) * inner] = (
                    (levels - offset * series) * back
                ).astype(jnp.bfloat16)

        for mask, peer in peers:
            q_copy(chunk, mask, peer).start()
        d_buf[chunk, place] = q_buf[chunk, me]

    def reduce_stage(chunk, stage):
        r_copy(chunk, stage).wait_recv()
        kept, sent, span = half_at(stage)
        last = stage == stages - 1
        columns = part.shape[3] // 4

        @pl.loop(0, span * 4)
        def _(at):
            block, column = at // 4, pl.ds(pl.multiple_of((at % 4) * columns, 128), columns)
            total = (
                part[chunk, kept + block, :, column].astype(jnp.float32)
                + recv_bufs[stage][chunk, block, :, column].astype(jnp.float32)
            ).astype(jnp.bfloat16)
            if last:
                out_ref[pl.ds(chunk * rows, rows), column] = total
            else:
                part[chunk, kept + block, :, column] = total

        if not last:
            r_copy(chunk, stage + 1).start()

    for turn in range(chunks + stages):
        if turn < chunks:
            for mask, peer in peers:
                q_copy(turn, mask, peer).wait_recv()

            @pl.loop(0, tiles)
            def _(at):
                step = turn * tiles + at
                weight_copy(step).wait()
                part[turn, :, :, pl.ds(pl.multiple_of(at * tile, 128), tile)] = (
                    jnp.dot(
                        d_buf[turn].reshape(groups * rows, width),
                        w_buf[step % WEIGHT_SLOTS],
                        preferred_element_type=jnp.float32,
                    )
                    .astype(jnp.bfloat16)
                    .reshape(groups, rows, tile)
                )

                @pl.when(step + WEIGHT_SLOTS < chunks * tiles)
                def _():
                    weight_copy(step + WEIGHT_SLOTS).start()

            r_copy(turn, 0).start()
        for stage in range(stages):
            chunk = turn - 1 - stage
            if 0 <= chunk < chunks:
                reduce_stage(chunk, stage)

    for chunk in range(chunks):
        for mask, peer in peers:
            x_copy(chunk, mask, peer).wait_send()
            q_copy(chunk, mask, peer).wait_send()
        for stage in range(stages):
            r_copy(chunk, stage).wait_send()


def shards(activations, down_weight):
    count_rows, width = activations.shape
    features = down_weight.shape[1]
    groups = lax.axis_size("tensor")
    stages = groups.bit_length() - 1
    own = count_rows // groups
    rows = 16
    chunks = own // rows
    tile = 512
    table = jnp.asarray(np.kron(sylvester(INNER), paley_matrix()), jnp.bfloat16)
    inner = table.shape[0]
    bf16, dma = jnp.bfloat16, pltpu.SemaphoreType.DMA
    body = functools.partial(
        kernel, groups, chunks, tile, 1.0 / math.sqrt(width * groups), sine_terms()
    )
    return pl.pallas_call(
        body,
        out_shape=jax.ShapeDtypeStruct((own, features), bf16),
        in_specs=[
            pl.BlockSpec(memory_space=pl.ANY),
            pl.BlockSpec(memory_space=pl.ANY),
            pl.BlockSpec(memory_space=pltpu.VMEM),
        ],
        out_specs=pl.BlockSpec(memory_space=pltpu.VMEM),
        scratch_shapes=[
            pltpu.VMEM((chunks, groups, rows, width), bf16),
            pltpu.VMEM((width // inner, groups, rows, inner), jnp.float32),
            pltpu.VMEM((chunks, groups, rows, width), bf16),
            pltpu.VMEM((chunks, groups, rows, width), bf16),
            pltpu.VMEM((chunks, groups, rows, features), bf16),
            pltpu.VMEM((WEIGHT_SLOTS, width, tile), bf16),
        ]
        + [
            pltpu.VMEM((chunks, groups >> (stage + 1), rows, features), bf16)
            for stage in range(stages)
        ]
        + [
            dma((chunks, groups)),
            dma((chunks, groups)),
            dma((chunks,)),
            dma((chunks, groups)),
            dma((chunks, groups)),
            dma((chunks, stages)),
            dma((chunks, stages)),
            dma((WEIGHT_SLOTS,)),
        ],
        compiler_params=pltpu.CompilerParams(
            collective_id=0, has_side_effects=True, vmem_limit_bytes=60 * 1024 * 1024
        ),
        name="rotate_quantize_project",
    )(activations, down_weight, table)


def solution(mesh):
    placed = (P("dp", "tensor"), P("tensor", None))
    return jax.shard_map(
        shards, mesh=mesh, in_specs=placed, out_specs=P(("dp", "tensor"), None), check_vma=False
    )
```

time: 474 us -> 247 us (0.52)
  blocking collectives: 253 us -> 0 us
  Pallas kernels: 0 us -> 245 us
  waiting for transfers between devices: 117 us -> 0 us
  matrix products: 62.6 us -> 0 us
  other arithmetic: 26.5 us -> 0 us
  between operations: 13.4 us -> 0.01 us
    all_to_all x2 -> x0, blocking collectives: 253 us -> none  [the longest x1 168 us: shards(): lax.all_to_all(blocks, 'tensor', split_axis=0, concat_axis=0, tiled=True)]
    pallas_call x0 -> x1, Pallas kernels: none -> 245 us  [shards(): pl.pallas_call(body, out_shape=jax.ShapeDtypeStruct((own, features), bf16...]
    reduce_scatter x1 -> x0, waiting for transfers between devices: 117 us -> none  [shards(): lax.psum_scatter(jnp.dot(dequant, down_weight, preferred_element_type=jnp...]
    dot_general x3 -> x0, matrix products: 62.6 us -> none  [the longest x1 30.4 us: shards(): jnp.dot(dequant, down_weight, preferred_element_type=jnp.float32)]
    convert_element_type x1 -> x0, other arithmetic: 26.5 us -> none  [quantize(): return (snapped * token_scale / 7.0).astype(jnp.bfloat16)]
  transfers between devices with their start and end apart: 1 -> 0, of which waited for: 1 -> 0; matrix products, arithmetic and copies ran while one was open for 0% -> 0% of each run, Pallas kernels for 0% -> 0%
where the time goes in v1:
time: 247 us
  Pallas kernels  245 us (99%)
    pallas_call x1, Pallas kernels, shards(): pl.pallas_call(body, out_shape=jax.ShapeDtypeStruct((own, features), bf16...  245 us

profile of v1, /device:TPU:0, one launch (start us, length us, event | category | flops | bytes accessed | tf_op | source)
XLA Modules:
  0.0 247.0 jit_solution(11847173656123850135)
XLA Ops:
  0.0 244.9 %rotate_quantize_project.1 = bf16[64,6144]{1,0:T(8,128)(2,1)} custom-call(bf16[512,3584]{1,0:T(8,128)(2,1)} %act_ref.1, bf16[3584,6144]{1,0:T(8,128)(2,1)} %weight_ref.1, bf16[896,896]{1,0:T(8,128)(2,1)} %constant.2.clone.table_ref), custom_call_target="tpu_custom_call" | custom-call | tf_op jit(solution)/shard_map/rotate_quantize_project/pallas_call | solution.py:297
  244.9 2.1 copy.5

commit v2 on v1

--- a/solution.py
+++ b/solution.py
@@ -10,7 +10,9 @@
 from jax.sharding import PartitionSpec as P
 
 INNER = 32
-WEIGHT_SLOTS = 3
+WEIGHT_SLOTS = 8
+SECTIONS = 6
+AHEAD = 2
 
 
 def paley_matrix():
@@ -96,6 +98,8 @@
     inner = table_ref.shape[0]
     subs = width // inner
     tiles = weight_ref.shape[1] // tile
+    section_tiles = tiles // SECTIONS
+    section_width = section_tiles * tile
     place = mirrored(me, groups)
     peers = [(mask, flipped(me, mask)) for mask in range(groups - 1, 0, -1)]
 
@@ -143,13 +147,14 @@
             sent = start + (1 - bit) * span
         return kept, sent, span
 
-    def r_copy(chunk, stage):
+    def r_copy(chunk, stage, section):
         kept, sent, span = half_at(stage)
+        column = pl.ds(section * section_width, section_width)
         return pltpu.make_async_remote_copy(
-            src_ref=part.at[chunk, pl.ds(sent, span)],
-            dst_ref=recv_bufs[stage].at[chunk],
-            send_sem=r_send.at[chunk, stage],
-            recv_sem=r_recv.at[chunk, stage],
+            src_ref=part.at[chunk, pl.ds(sent, span), :, column],
+            dst_ref=recv_bufs[stage].at[chunk, :, :, column],
+            send_sem=r_send.at[chunk, stage, section],
+            recv_sem=r_recv.at[chunk, stage, section],
             device_id={"tensor": flipped(me, 1 << stage)},
             device_id_type=pl.DeviceIdType.MESH,
         )
@@ -161,18 +166,17 @@
         )
     pl.semaphore_wait(barrier, groups - 1)
 
-    for chunk in range(chunks):
+    def exchange(chunk):
         for mask, peer in peers:
             x_copy(chunk, mask, peer).start()
         own_rows(chunk).start()
+
+    for chunk in range(min(AHEAD, chunks)):
+        exchange(chunk)
     for step in range(WEIGHT_SLOTS):
         weight_copy(step).start()
 
-    @pl.loop(0, chunks)
-    def _(chunk):
-        own_rows(chunk).wait()
-        for mask, peer in peers:
-            x_copy(chunk, mask, peer).wait_recv()
+    def rotate(chunk):
         for sub in range(subs):
             block = x_buf[chunk, :, :, sub * inner:(sub + 1) * inner]
             rot[sub] = jnp.dot(
@@ -217,19 +221,27 @@
                     (levels - offset * series) * back
                 ).astype(jnp.bfloat16)
 
+    def finish_tokens(chunk):
+        own_rows(chunk).wait()
+        for mask, peer in peers:
+            x_copy(chunk, mask, peer).wait_recv()
+        rotate(chunk)
         for mask, peer in peers:
             q_copy(chunk, mask, peer).start()
         d_buf[chunk, place] = q_buf[chunk, me]
-
-    def reduce_stage(chunk, stage):
-        r_copy(chunk, stage).wait_recv()
+        if chunk + AHEAD < chunks:
+            exchange(chunk + AHEAD)
+
+    def reduce_stage(chunk, stage, section):
+        r_copy(chunk, stage, section).wait_recv()
         kept, sent, span = half_at(stage)
         last = stage == stages - 1
-        columns = part.shape[3] // 4
-
-        @pl.loop(0, span * 4)
+        piece = section_width // 2
+
+        @pl.loop(0, span * 2)
         def _(at):
-            block, column = at // 4, pl.ds(pl.multiple_of((at % 4) * columns, 128), columns)
+            block = at // 2
+            column = pl.ds(pl.multiple_of(section * section_width + (at % 2) * piece, 128), piece)
             total = (
                 part[chunk, kept + block, :, column].astype(jnp.float32)
                 + recv_bufs[stage][chunk, block, :, column].astype(jnp.float32)
@@ -240,20 +252,19 @@
                 part[chunk, kept + block, :, column] = total
 
         if not last:
-            r_copy(chunk, stage + 1).start()
-
-    for turn in range(chunks + stages):
-        if turn < chunks:
-            for mask, peer in peers:
-                q_copy(turn, mask, peer).wait_recv()
-
-            @pl.loop(0, tiles)
+            r_copy(chunk, stage + 1, section).start()
+
+    def project(chunk):
+        for mask, peer in peers:
+            q_copy(chunk, mask, peer).wait_recv()
+        for section in range(SECTIONS):
+            @pl.loop(section * section_tiles, (section + 1) * section_tiles)
             def _(at):
-                step = turn * tiles + at
+                step = chunk * tiles + at
                 weight_copy(step).wait()
-                part[turn, :, :, pl.ds(pl.multiple_of(at * tile, 128), tile)] = (
+                part[chunk, :, :, pl.ds(pl.multiple_of(at * tile, 128), tile)] = (
                     jnp.dot(
-                        d_buf[turn].reshape(groups * rows, width),
+                        d_buf[chunk].reshape(groups * rows, width),
                         w_buf[step % WEIGHT_SLOTS],
                         preferred_element_type=jnp.float32,
                     )
@@ -265,18 +276,28 @@
                 def _():
                     weight_copy(step + WEIGHT_SLOTS).start()
 
-            r_copy(turn, 0).start()
+            r_copy(chunk, 0, section).start()
+
+    for chunk in range(min(AHEAD, chunks)):
+        finish_tokens(chunk)
+    for turn in range(chunks + stages):
+        if turn < chunks:
+            project(turn)
         for stage in range(stages):
             chunk = turn - 1 - stage
             if 0 <= chunk < chunks:
-                reduce_stage(chunk, stage)
+                for section in range(SECTIONS):
+                    reduce_stage(chunk, stage, section)
+        if AHEAD <= turn + AHEAD < chunks:
+            finish_tokens(turn + AHEAD)
 
     for chunk in range(chunks):
         for mask, peer in peers:
             x_copy(chunk, mask, peer).wait_send()
             q_copy(chunk, mask, peer).wait_send()
         for stage in range(stages):
-            r_copy(chunk, stage).wait_send()
+            for section in range(SECTIONS):
+                r_copy(chunk, stage, section).wait_send()
 
 
 def shards(activations, down_weight):
@@ -321,8 +342,8 @@
             dma((chunks,)),
             dma((chunks, groups)),
             dma((chunks, groups)),
-            dma((chunks, stages)),
-            dma((chunks, stages)),
+            dma((chunks, stages, SECTIONS)),
+            dma((chunks, stages, SECTIONS)),
             dma((WEIGHT_SLOTS,)),
         ],
         compiler_params=pltpu.CompilerParams(

time: 247 us -> 213 us (0.86)
  Pallas kernels: 245 us -> 210 us
    pallas_call x1, Pallas kernels: 245 us -> 210 us  [shards(): pl.pallas_call(body, out_shape=jax.ShapeDtypeStruct((own, features), bf16...]
where the time goes in v2:
time: 213 us; the launch traced here: 212 us
  Pallas kernels  210 us (99%)
    pallas_call x1, Pallas kernels, shards(): pl.pallas_call(body, out_shape=jax.ShapeDtypeStruct((own, features), bf16...  210 us

profile of v2, /device:TPU:0, one launch (start us, length us, event | category | flops | bytes accessed | tf_op | source)
XLA Modules:
  0.0 212.4 jit_solution(14519173111976821401)
XLA Ops:
  0.0 210.4 %rotate_quantize_project.1 = bf16[64,6144]{1,0:T(8,128)(2,1)} custom-call(bf16[512,3584]{1,0:T(8,128)(2,1)} %act_ref.1, bf16[3584,6144]{1,0:T(8,128)(2,1)} %weight_ref.1, bf16[896,896]{1,0:T(8,128)(2,1)} %constant.2.clone.table_ref), custom_call_target="tpu_custom_call" | custom-call | tf_op jit(solution)/shard_map/rotate_quantize_project/pallas_call | solution.py:318
  210.4 2.1 copy.5

commit v3 on v2

--- a/solution.py
+++ b/solution.py
@@ -283,10 +283,10 @@
     for turn in range(chunks + stages):
         if turn < chunks:
             project(turn)
-        for stage in range(stages):
-            chunk = turn - 1 - stage
-            if 0 <= chunk < chunks:
-                for section in range(SECTIONS):
+        for section in range(SECTIONS):
+            for stage in range(stages - 1, -1, -1):
+                chunk = turn - 1 - stage
+                if 0 <= chunk < chunks:
                     reduce_stage(chunk, stage, section)
         if AHEAD <= turn + AHEAD < chunks:
             finish_tokens(turn + AHEAD)

time: 213 us -> 213 us (level)
  no operation moved by 1% of the time
where the time goes in v3:
time: 213 us
  Pallas kernels  211 us (99%)
    pallas_call x1, Pallas kernels, shards(): pl.pallas_call(body, out_shape=jax.ShapeDtypeStruct((own, features), bf16...  211 us

profile of v3, /device:TPU:0, one launch (start us, length us, event | category | flops | bytes accessed | tf_op | source)
XLA Modules:
  0.0 212.9 jit_solution(12171017812361381049)
XLA Ops:
  0.0 210.9 %rotate_quantize_project.1 = bf16[64,6144]{1,0:T(8,128)(2,1)} custom-call(bf16[512,3584]{1,0:T(8,128)(2,1)} %act_ref.1, bf16[3584,6144]{1,0:T(8,128)(2,1)} %weight_ref.1, bf16[896,896]{1,0:T(8,128)(2,1)} %constant.2.clone.table_ref), custom_call_target="tpu_custom_call" | custom-call | tf_op jit(solution)/shard_map/rotate_quantize_project/pallas_call | solution.py:318
  210.9 2.1 copy.5
